TPU v7x, 32 devices: a whole 2x2x4 slice. The times are simulated.
32 devices in a mesh: gx: 4 (over z), gy: 8 (over y, x, core).
Axes of the slice: x: 2, y: 2, z: 4, core: 2. Of those that a mesh axis runs over, the one named last changes fastest.
Arguments:
- coordinates: float32 [3, 65536], P(None, ('gx', 'gy')), may hold values from 0 to 1
- rhs: float32 [16, 65536], P(None, ('gx', 'gy')), may hold values from -70 to 70
- leaf_order: int32 [32, 2048], P(('gx', 'gy')), may hold values from 0 to 2047, each once within a row
- leaf_sizes: int32 [32], P(('gx', 'gy')), may hold values from 1 to 2048, 49152 in all
- inverse_scales: float32 [3], replicated, may hold values from 12 to 30
- noise_var: float32 [1], replicated, may hold values from 0.3 to 1
- u_factors: float32 [5, 64, 65536], P(None, None, ('gx', 'gy')), may hold values from -0.375 to 0.375
- v_factors: float32 [5, 64, 65536], P(None, None, ('gx', 'gy')), may hold values from -1 to 1
Outputs:
- solution: float32 [16, 65536], P(None, ('gx', 'gy'))
Inputs may be any that keep to these rules, and one draw needn't show every extreme that they name: `leaf_sizes`: each leaf's live points stand first in leaf order.
All inputs are finite; a program needn't handle non-finite values. No bound on the sum of `leaf_sizes` on one device may be relied on, other than what follows from the above.
Results may differ from a plain program's by a relative error of at most 0.0001.
Values sent between devices are 32-bit elements; how exact they have to be, the bound alone decides.
A program may use at most 128 MiB of HBM per device.

v0:
```python
import functools
import math

import jax
import jax.numpy as jnp
from jax import lax
from jax.experimental import pallas as pl
from jax.experimental.pallas import tpu as pltpu
from jax.sharding import PartitionSpec as P

ITERS = 3

epsilon = 1e-06
sqrt_three = math.sqrt(3.0)
log2_e = math.log2(math.e)
MESH = pl.DeviceIdType.MESH
f32 = jnp.float32
bf16 = jnp.bfloat16
NN = (((1,), (0,)), ((), ()))
NT = (((1,), (1,)), ((), ()))


def least_squares(columns, beta):
    count_cols = len(columns)
    cosines = []
    sines = []
    target = [beta] + [jnp.zeros_like(beta)] * count_cols
    upper = []
    for column_idx in range(count_cols):
        entries = list(columns[column_idx])
        for row_idx in range(column_idx):
            first_val = entries[row_idx]
            second_val = entries[row_idx + 1]
            entries[row_idx] = cosines[row_idx] * first_val + sines[row_idx] * second_val
            entries[row_idx + 1] = -sines[row_idx] * first_val + cosines[row_idx] * second_val
        first_val = entries[column_idx]
        second_val = entries[column_idx + 1]
        radius = jnp.sqrt(first_val * first_val + second_val * second_val)
        cosines.append(first_val / radius)
        sines.append(second_val / radius)
        entries[column_idx] = radius
        carried = target[column_idx]
        target[column_idx] = cosines[column_idx] * carried
        target[column_idx + 1] = -sines[column_idx] * carried
        upper.append(entries[: column_idx + 1])
    weights = [None] * count_cols
    for column_idx in reversed(range(count_cols)):
        accum = target[column_idx]
        for later_idx in range(column_idx + 1, count_cols):
            accum = accum - upper[later_idx][column_idx] * weights[later_idx]
        weights[column_idx] = accum / upper[column_idx][column_idx]
    return weights


def flipped(index, bits):
    result = index
    place = 1
    while place <= bits:
        if bits & place:
            result = result + place * (1 - 2 * lax.rem(lax.div(index, place), 2))
        place *= 2
    return result


def split2(value):
    high = value.astype(bf16)
    low = (value - high.astype(f32)).astype(bf16)
    return high, low


def split3(value):
    high = value.astype(bf16)
    rest = value - high.astype(f32)
    mid = rest.astype(bf16)
    low = (rest - mid.astype(f32)).astype(bf16)
    return high, mid, low


def dot(left, right, dims=NN):
    return lax.dot_general(left, right, dims, preferred_element_type=f32)


def fused(
    size_gx, size_gy,
    coords_ref, rhs_ref, order_ref, sizes_ref, inv_ref, noise_ref, u_hbm, v_hbm,
    out_ref,
    near_hi, near_lo, columns_pos, rows_pos, u_raw, v_raw, u_hi, u_lo, v_hi, v_lo,
    basis_ref, image_ref,
    send_part, recv_low, recv_high, send_node, recv_node,
    send_dots, recv_dots,
    load_sem,
    part_s, part_r, node_s, node_r, dots_s, dots_r,
):
    me_x = lax.axis_index("gx")
    me_y = lax.axis_index("gy")
    levels_low = size_gy.bit_length() - 1
    levels_high = size_gx.bit_length() - 1
    nv, leaf_len = rhs_ref.shape
    num_dims = coords_ref.shape[0]
    num_levels, num_rank = u_raw.shape[0], u_raw.shape[1]
    half = nv // 2
    lanes = 2 * num_rank
    size_all = size_gx * size_gy

    u_load = pltpu.make_async_copy(u_hbm, u_raw, load_sem.at[0])
    v_load = pltpu.make_async_copy(v_hbm, v_raw, load_sem.at[1])
    v_load.start()
    u_load.start()

    peers = [
        (flipped(me_x, apart // size_gy), flipped(me_y, apart % size_gy)) for apart in range(size_all)
    ]
    barrier = pltpu.get_barrier_semaphore()
    for apart in range(1, size_all):
        pl.semaphore_signal(barrier, inc=1, device_id=peers[apart], device_id_type=MESH)

    def send(src, dst, sems, semr, device):
        copy = pltpu.make_async_remote_copy(
            src_ref=src, dst_ref=dst, send_sem=sems, recv_sem=semr,
            device_id=device, device_id_type=MESH,
        )
        copy.start()
        return copy

    live = jnp.where(
        lax.broadcasted_iota(jnp.int32, (1, leaf_len), 1) < sizes_ref[0], 1.0, 0.0
    ).astype(f32)

    width = 128
    groups = leaf_len // width
    order = order_ref[...]
    outer = lax.div(order, width)
    inner = order - outer * width
    pick = jnp.where(
        lax.broadcasted_iota(jnp.int32, (width, leaf_len), 0) == inner, 1.0, 0.0
    ).astype(bf16)

    def gather(value):
        rows = value.shape[0]
        parts = []
        for part in split3(value):
            parts += [part[:, g * width : (g + 1) * width] for g in range(groups)]
        stacked = jnp.concatenate(parts, axis=0)
        pieces = []
        for start_col in range(0, leaf_len, 512):
            cols = slice(start_col, start_col + 512)
            got = dot(stacked, pick[:, cols])
            total = jnp.zeros((rows, 512), f32)
            for g in range(groups):
                terms = [
                    got[(part * groups + g) * rows : (part * groups + g + 1) * rows] for part in range(3)
                ]
                total = jnp.where(outer[:, cols] == g, terms[0] + terms[1] + terms[2], total)
            pieces.append(total)
        return jnp.concatenate(pieces, axis=1)

    pad = jnp.zeros((16 - num_dims, leaf_len), f32)
    row_sel = lax.broadcasted_iota(jnp.int32, (16, 1), 0)
    scale = jnp.zeros((16, 1), f32)
    for dim in range(num_dims):
        scale = jnp.where(row_sel == dim, inv_ref[dim], scale)
    gathered = gather(jnp.concatenate([coords_ref[...], pad], axis=0))
    rows_pos[0:16, :] = gathered * scale * sqrt_three
    rows_pos[16:, :] = jnp.zeros((rows_pos.shape[0] - 16, leaf_len), f32)
    columns_pos[...] = rows_pos[...].T
    basis_ref[0] = live * gather(rhs_ref[...])

    padded = v_hi.shape[0]
    used = num_levels * num_rank

    def prepare(raw, hi, lo):
        for level in range(num_levels):
            first, second = split2(raw[level])
            hi[level * num_rank : (level + 1) * num_rank, :] = first
            lo[level * num_rank : (level + 1) * num_rank, :] = second
        if padded > used:
            hi[used:, :] = jnp.zeros((padded - used, leaf_len), bf16)
            lo[used:, :] = jnp.zeros((padded - used, leaf_len), bf16)

    lane = lax.broadcasted_iota(jnp.int32, (half, lanes), 1)
    left_side = lane < num_rank

    def swap(value):
        return pltpu.roll(value, num_rank, 1)

    def send_partials(it, coef):
        for level in range(num_levels):
            block = coef[:, (level // 2) * lanes : (level // 2 + 1) * lanes]
            top, bottom = block[:half], block[half:]
            if level % 2 == 0:
                tile = jnp.where(left_side, top, swap(bottom))
            else:
                tile = jnp.where(left_side, swap(top), bottom)
            send_part[it, level] = tile
        copies = []
        for apart in range(1, size_gy):
            copies.append(send(
                send_part.at[it, pl.ds(levels_low, levels_high)], recv_high.at[it, apart],
                part_s.at[it, apart, 1], part_r.at[it, apart, 1], peers[apart],
            ))
        late = []
        for apart in range(1, size_gy):
            late.append(send(
                send_part.at[it, apart.bit_length() - 1], recv_low.at[it, apart],
                part_s.at[it, apart, 0], part_r.at[it, apart, 0], peers[apart],
            ))
        return copies, late

    def send_nodes(it, part_copies):
        for copy in part_copies:
            copy.wait_recv()
        total = send_part[it, levels_low:num_levels]
        for apart in range(1, size_gy):
            total = total + recv_high[it, apart]
        send_node[it] = total
        return [
            send(
                send_node.at[it, apart.bit_length() - 1], recv_node.at[it, apart],
                node_s.at[it, apart], node_r.at[it, apart], peers[apart * size_gy],
            )
            for apart in range(1, size_gx)
        ]

    def siblings(it, copies):
        for copy in copies:
            copy.wait_recv()
        tiles = []
        for count, source in ((levels_low, recv_low), (levels_high, recv_node)):
            for level in range(count):
                total = source[it, 2**level]
                for apart in range(2**level + 1, 2 ** (level + 1)):
                    total = total + source[it, apart]
                tiles.append(total)
        if len(tiles) % 2:
            tiles.append(jnp.zeros_like(tiles[0]))
        blocks = []
        for pair in range(len(tiles) // 2):
            even, odd = tiles[2 * pair], tiles[2 * pair + 1]
            top = jnp.where(left_side, even, swap(odd))
            bottom = jnp.where(left_side, swap(even), odd)
            blocks.append(jnp.concatenate([top, bottom], axis=0))
        return jnp.concatenate(blocks, axis=1)

    slots = lanes // nv
    row16 = lax.broadcasted_iota(jnp.int32, (nv, lanes), 0)
    slot16 = lax.broadcasted_iota(jnp.int32, (nv, lanes), 1) - row16 * slots

    def send_sums(it, values):
        block = jnp.zeros((nv, lanes), f32)
        for idx, value in enumerate(values):
            block = jnp.where(slot16 == idx, value, block)
        send_dots[it] = jnp.sum(block, axis=0, keepdims=True)
        return [
            send(
                send_dots.at[it], recv_dots.at[it, apart],
                dots_s.at[it, apart], dots_r.at[it, apart], peers[apart],
            )
            for apart in range(1, size_all)
        ]

    def read_sums(it, copies, count):
        for copy in copies:
            copy.wait_recv()
        terms = [send_dots[it]] + [recv_dots[it, apart] for apart in range(1, size_all)]
        while len(terms) > 1:
            terms = [terms[i] + terms[i + 1] for i in range(0, len(terms), 2)]
        return [
            jnp.sum(jnp.where(slot16 == idx, terms[0], 0.0), axis=1, keepdims=True)
            for idx in range(count)
        ]

    chunk = min(512, leaf_len)

    def near_columns(both, first, begin, end):
        for low in range(begin, end, chunk):
            high = low + chunk
            cols = slice(low, high)
            wide = dot(both[:, :high], near_hi[:high, cols])
            rest = dot(first[:, :high], near_lo[:high, cols])
            if high < leaf_len:
                wide = wide + dot(both[:, high:], near_hi[cols, high:], NT)
                rest = rest + dot(first[:, high:], near_lo[cols, high:], NT)
            image_ref[:, cols] = wide[:nv] + wide[nv:] + rest

    rows = 16

    def fill_near(begin, end):
        for low in range(begin, end, chunk):
            cols = slice(low, low + chunk)

            def fill(block, carry, cols=cols):
                base = pl.multiple_of(block * rows, rows)
                square = None
                for dim in range(num_dims):
                    differ = columns_pos[pl.ds(base, rows), dim : dim + 1] - rows_pos[dim : dim + 1, cols]
                    square = differ * differ if square is None else square + differ * differ
                distance = square * lax.rsqrt(jnp.maximum(square, 1e-30))
                value = (1.0 + distance) * jnp.exp2(distance * (-log2_e))
                hi, lo = split2(value)
                near_hi[pl.ds(base, rows), cols] = hi
                near_lo[pl.ds(base, rows), cols] = lo
                return carry

            lax.fori_loop(0, (low + chunk) // rows, fill, 0, unroll=16)

    pending = []

    def operate(it, vector):
        first, second = split2(vector)
        both = jnp.concatenate([first, second], axis=0)
        if it == 0:
            v_load.wait()
            prepare(v_raw, v_hi, v_lo)
        wide = dot(both, v_hi[...], NT)
        coef = wide[:nv] + wide[nv:] + dot(first, v_lo[...], NT)
        if it == 0:
            pl.semaphore_wait(barrier, size_all - 1)
        parts, late = send_partials(it, coef)
        if it == 0:
            fill_near(0, leaf_len - chunk)
            nodes = send_nodes(it, parts)
            fill_near(leaf_len - chunk, leaf_len)
            u_load.wait()
            prepare(u_raw, u_hi, u_lo)
            near_columns(both, first, 0, leaf_len)
        else:
            near_columns(both, first, 0, leaf_len // 2)
            nodes = send_nodes(it, parts)
            near_columns(both, first, leaf_len // 2, leaf_len)
        coef_hi, coef_lo = split2(siblings(it, late + nodes))
        wide = dot(jnp.concatenate([coef_hi, coef_lo], axis=0), u_hi[...])
        far = wide[:nv] + wide[nv:] + dot(coef_hi, u_lo[...])
        pending.extend(parts + late + nodes)
        return live * (image_ref[...] + far) - vector

    def lane_sum(value):
        return jnp.sum(value, axis=1, keepdims=True)

    shift = 1.0 + noise_ref[0]
    gram = {}
    columns = []
    images = []
    beta = None
    raw = basis_ref[0]
    image = operate(0, raw)
    for it in range(ITERS):
        last = it + 1 == ITERS
        values = [lane_sum(basis_ref[row] * image) for row in range(it)] + [lane_sum(raw * image)]
        values += [lane_sum(basis_ref[row] * raw) for row in range(it)] + [lane_sum(raw * raw)]
        if last:
            values.append(lane_sum(image * image))
        copies = send_sums(it, values)
        if last:
            for copy in pending:
                copy.wait_send()
            pending = []
            ahead = None
        else:
            ahead = operate(it + 1, image)
        pending.extend(copies)
        sums = read_sums(it, copies, len(values))
        length = jnp.sqrt(sums[2 * it + 1] + epsilon)
        inverse = 1.0 / length
        if it == 0:
            beta = length
        else:
            columns[-1].append(length)
        products = [value * inverse for value in sums[: it + 1]]
        products[it] = products[it] * inverse
        lengths = [value * inverse for value in sums[it + 1 : 2 * it + 2]]
        lengths[it] = lengths[it] * inverse
        vector = raw * inverse
        basis_ref[it] = vector
        for row in range(it + 1):
            gram[row, it] = gram[it, row] = lengths[row]
        column = [products[row] + shift * lengths[row] for row in range(it + 1)]
        moved = [column[row] - shift if row == it else column[row] for row in range(it + 1)]
        columns.append(list(column))
        if last:
            rest = sums[-1] * inverse * inverse
            for row in range(it + 1):
                inside = -2.0 * products[row]
                for other in range(it + 1):
                    inside = inside + moved[other] * gram[row, other]
                rest = rest + moved[row] * inside
            columns[-1].append(jnp.sqrt(jnp.maximum(rest, 0.0) + epsilon))
        else:
            images.append(image * inverse)
            raw = images[it]
            image = ahead * inverse
            for row in range(it + 1):
                raw = raw - moved[row] * basis_ref[row]
                image = image - moved[row] * images[row]
    weights = least_squares(columns, beta)
    solved = weights[0] * basis_ref[0]
    for it in range(1, ITERS):
        solved = solved + weights[it] * basis_ref[it]
    parts = split3(solved)
    for g in range(groups):
        mask = jnp.where(outer == g, 1.0, 0.0).astype(bf16)
        stacked = jnp.concatenate([part * mask for part in parts], axis=0)
        got = dot(stacked, pick, NT)
        out_ref[:, g * width : (g + 1) * width] = got[:nv] + got[nv : 2 * nv] + got[2 * nv :]
    for copy in pending:
        copy.wait_send()


def per_device(
    size_gx, size_gy,
    coordinates, rhs, leaf_order, leaf_sizes, inverse_scales, noise_var, u_factors, v_factors,
):
    num_vectors, leaf_len = rhs.shape
    num_levels, num_rank = u_factors.shape[0], u_factors.shape[1]
    levels_high = size_gx.bit_length() - 1
    half, lanes = num_vectors // 2, 2 * num_rank
    padded = (num_levels + 1) // 2 * 2 * num_rank
    tile = (half, lanes)
    vmem = pl.BlockSpec(memory_space=pltpu.VMEM)
    smem = pl.BlockSpec(memory_space=pltpu.SMEM)
    any_space = pl.BlockSpec(memory_space=pl.ANY)
    dma = pltpu.SemaphoreType.DMA
    return pl.pallas_call(
        functools.partial(fused, size_gx, size_gy),
        out_shape=jax.ShapeDtypeStruct(rhs.shape, f32),
        in_specs=[vmem, vmem, vmem, smem, smem, smem, any_space, any_space],
        out_specs=vmem,
        scratch_shapes=[
            pltpu.VMEM((leaf_len, leaf_len), bf16),
            pltpu.VMEM((leaf_len, leaf_len), bf16),
            pltpu.VMEM((leaf_len, 128), f32),
            pltpu.VMEM((128, leaf_len), f32),
            pltpu.VMEM(u_factors.shape, f32),
            pltpu.VMEM(v_factors.shape, f32),
            pltpu.VMEM((padded, leaf_len), bf16),
            pltpu.VMEM((padded, leaf_len), bf16),
            pltpu.VMEM((padded, leaf_len), bf16),
            pltpu.VMEM((padded, leaf_len), bf16),
            pltpu.VMEM((ITERS,) + rhs.shape, f32),
            pltpu.VMEM(rhs.shape, f32),
            pltpu.VMEM((ITERS, num_levels) + tile, f32),
            pltpu.VMEM((ITERS, size_gy) + tile, f32),
            pltpu.VMEM((ITERS, size_gy, levels_high) + tile, f32),
            pltpu.VMEM((ITERS, levels_high) + tile, f32),
            pltpu.VMEM((ITERS, size_gx) + tile, f32),
            pltpu.VMEM((ITERS, 1, lanes), f32),
            pltpu.VMEM((ITERS, size_gx * size_gy, 1, lanes), f32),
            dma((2,)),
            dma((ITERS, size_gy, 2)),
            dma((ITERS, size_gy, 2)),
            dma((ITERS, size_gx)),
            dma((ITERS, size_gx)),
            dma((ITERS, size_gx * size_gy)),
            dma((ITERS, size_gx * size_gy)),
        ],
        compiler_params=pltpu.CompilerParams(collective_id=0, has_side_effects=True),
        name="gmres",
    )(coordinates, rhs, leaf_order, leaf_sizes, inverse_scales, noise_var, u_factors, v_factors)


def solution(mesh):
    in_specs = (
        P(None, ("gx", "gy")),
        P(None, ("gx", "gy")),
        P(("gx", "gy"), None),
        P(("gx", "gy")),
        P(),
        P(),
        P(None, None, ("gx", "gy")),
        P(None, None, ("gx", "gy")),
    )
    out_specs = P(None, ("gx", "gy"))
    return jax.shard_map(
        functools.partial(per_device, mesh.shape["gx"], mesh.shape["gy"]),
        mesh=mesh, in_specs=in_specs, out_specs=out_specs, check_vma=False,
    )
```

profile of v0, /device:TPU:0, one launch (start us, length us, event | category | flops | bytes accessed | tf_op | source)
XLA Modules:
  0.0 53.0 jit_solution(13185891897047487705)
XLA Ops:
  1.3 50.1 %gmres.1 = f32[16,2048]{1,0:T(8,128)} custom-call(f32[3,2048]{1,0:T(4,128)} %coords_ref.1, f32[16,2048]{1,0:T(8,128)} %rhs_ref.1, s32[1,2048]{1,0:T(1,128)} %order_ref.1, s32[1]{0:T(128)S(6)} %copy.10.sizes_ref, f32[3]{0:T(128)} %inv_ref.1, f32[1]{0:T(128)S(6)} %copy.11.noise_ref, f32[5,64,2048]{2,1,0:T(8,128)} %u_hbm.1, f32[5,64,2048]{2,1,0:T(8,128)} %v_hbm.1), custom_call_target="tpu_custom_call" | custom-call | tf_op jit(solution)/shard_map/gmres/pallas_call | solution.py:422
  51.4 1.6 %copy.12 = f32[16,2048]{1,0:T(8,128)} copy(f32[16,2048]{1,0:T(8,128)} %gmres.1) | data formatting | bytes 262144
where the time goes:
time: 53.1 us; the launch traced here: 53 us
  Pallas kernels  50.1 us (94%)
  local copies, waits for them, and re-layouts  1.57 us (3%)
  between operations  1.31 us (2%)
    pallas_call x1, Pallas kernels, per_device(): pl.pallas_call(functools.partial(fused, size_gx, size_gy), out_shape=jax....  50.1 us
    unnamed x1, local copies, waits for them, and re-layouts  1.57 us

commit v1 on v0

v1 whole, which is shorter than its diff:
```python
import contextlib
import functools
import math

import jax
import jax.numpy as jnp
from jax import lax
from jax.experimental import pallas as pl
from jax.experimental.pallas import tpu as pltpu
from jax.sharding import PartitionSpec as P

ITERS = 3

epsilon = 1e-06
sqrt_three = math.sqrt(3.0)
log2_e = math.log2(math.e)
MESH = pl.DeviceIdType.MESH
f32 = jnp.float32
bf16 = jnp.bfloat16
NN = (((1,), (0,)), ((), ()))
NT = (((1,), (1,)), ((), ()))


def least_squares(columns, beta):
    count_cols = len(columns)
    cosines = []
    sines = []
    target = [beta] + [jnp.zeros_like(beta)] * count_cols
    upper = []
    for column_idx in range(count_cols):
        entries = list(columns[column_idx])
        for row_idx in range(column_idx):
            first_val = entries[row_idx]
            second_val = entries[row_idx + 1]
            entries[row_idx] = cosines[row_idx] * first_val + sines[row_idx] * second_val
            entries[row_idx + 1] = -sines[row_idx] * first_val + cosines[row_idx] * second_val
        first_val = entries[column_idx]
        second_val = entries[column_idx + 1]
        radius = jnp.sqrt(first_val * first_val + second_val * second_val)
        cosines.append(first_val / radius)
        sines.append(second_val / radius)
        entries[column_idx] = radius
        carried = target[column_idx]
        target[column_idx] = cosines[column_idx] * carried
        target[column_idx + 1] = -sines[column_idx] * carried
        upper.append(entries[: column_idx + 1])
    weights = [None] * count_cols
    for column_idx in reversed(range(count_cols)):
        accum = target[column_idx]
        for later_idx in range(column_idx + 1, count_cols):
            accum = accum - upper[later_idx][column_idx] * weights[later_idx]
        weights[column_idx] = accum / upper[column_idx][column_idx]
    return weights


def flipped(index, bits):
    result = index
    place = 1
    while place <= bits:
        if bits & place:
            result = result + place * (1 - 2 * lax.rem(lax.div(index, place), 2))
        place *= 2
    return result


def split2(value):
    high = value.astype(bf16)
    low = (value - high.astype(f32)).astype(bf16)
    return high, low


def split3(value):
    high = value.astype(bf16)
    rest = value - high.astype(f32)
    mid = rest.astype(bf16)
    low = (rest - mid.astype(f32)).astype(bf16)
    return high, mid, low


@contextlib.contextmanager
def phase(name):
    pl.delay(1)
    with jax.named_scope(name):
        yield
    pl.delay(1)


def dot(left, right, dims=NN):
    return lax.dot_general(left, right, dims, preferred_element_type=f32)


def fused(
    size_gx, size_gy,
    coords_ref, rhs_ref, order_ref, sizes_ref, inv_ref, noise_ref, u_hbm, v_hbm,
    out_ref,
    near_hi, near_lo, pick_ref, left_ref, right_ref, u_raw, v_raw, u_hi, u_lo, v_hi, v_lo,
    basis_ref, image_ref,
    send_part, recv_low, recv_high, send_node, recv_node,
    send_dots, recv_dots,
    load_sem,
    part_s, part_r, node_s, node_r, dots_s, dots_r,
):
    me_x = lax.axis_index("gx")
    me_y = lax.axis_index("gy")
    levels_low = size_gy.bit_length() - 1
    levels_high = size_gx.bit_length() - 1
    nv, leaf_len = rhs_ref.shape
    num_dims = coords_ref.shape[0]
    num_levels, num_rank = u_raw.shape[0], u_raw.shape[1]
    half = nv // 2
    lanes = 2 * num_rank
    size_all = size_gx * size_gy

    u_load = pltpu.make_async_copy(u_hbm, u_raw, load_sem.at[0])
    v_load = pltpu.make_async_copy(v_hbm, v_raw, load_sem.at[1])
    v_load.start()
    u_load.start()

    peers = [
        (flipped(me_x, apart // size_gy), flipped(me_y, apart % size_gy)) for apart in range(size_all)
    ]
    barrier = pltpu.get_barrier_semaphore()
    for apart in range(1, size_all):
        pl.semaphore_signal(barrier, inc=1, device_id=peers[apart], device_id_type=MESH)

    def send(src, dst, sems, semr, device):
        copy = pltpu.make_async_remote_copy(
            src_ref=src, dst_ref=dst, send_sem=sems, recv_sem=semr,
            device_id=device, device_id_type=MESH,
        )
        copy.start()

    def landed(block, sem):
        pltpu.make_async_copy(block, block, sem).wait()

    live = jnp.where(
        lax.broadcasted_iota(jnp.int32, (1, leaf_len), 1) < sizes_ref[0], 1.0, 0.0
    ).astype(f32)

    width = 256
    groups = leaf_len // width
    order = order_ref[...]
    outer = lax.div(order, width)
    inner = order - outer * width
    with phase("onehot"):
        pick_ref[...] = jnp.where(
            lax.broadcasted_iota(jnp.int32, (width, leaf_len), 0) == inner, 1.0, 0.0
        ).astype(bf16)
    def gather(stack, pieces):
        rows = stack.shape[0] // pieces
        stacked = jnp.concatenate([stack[:, g * width : (g + 1) * width] for g in range(groups)], axis=0)
        blocks = []
        for start_col in range(0, leaf_len, 512):
            cols = slice(start_col, start_col + 512)
            got = dot(stacked, pick_ref[:, cols])
            total = jnp.zeros((rows, 512), f32)
            for g in range(groups):
                term = None
                for piece in range(pieces):
                    base = (g * pieces + piece) * rows
                    term = got[base : base + rows] if term is None else term + got[base : base + rows]
                total = jnp.where(outer[:, cols] == g, term, total)
            blocks.append(total)
        return jnp.concatenate(blocks, axis=1)

    with phase("gather_rhs"):
        basis_ref[0] = live * gather(jnp.concatenate(split3(rhs_ref[...]), axis=0), 3)

    padded = v_hi.shape[0]
    used = num_levels * num_rank

    def prepare(raw, hi, lo):
        for level in range(num_levels):
            first, second = split2(raw[level])
            hi[level * num_rank : (level + 1) * num_rank, :] = first
            lo[level * num_rank : (level + 1) * num_rank, :] = second
        if padded > used:
            hi[used:, :] = jnp.zeros((padded - used, leaf_len), bf16)
            lo[used:, :] = jnp.zeros((padded - used, leaf_len), bf16)

    lane = lax.broadcasted_iota(jnp.int32, (half, lanes), 1)
    left_side = lane < num_rank

    def swap(value):
        return pltpu.roll(value, num_rank, 1)

    def send_partials(it, coef):
        for level in range(num_levels):
            block = coef[:, (level // 2) * lanes : (level // 2 + 1) * lanes]
            top, bottom = block[:half], block[half:]
            if level % 2 == 0:
                tile = jnp.where(left_side, top, swap(bottom))
            else:
                tile = jnp.where(left_side, swap(top), bottom)
            send_part[it, level] = tile
        for apart in range(1, size_gy):
            send(
                send_part.at[it, pl.ds(levels_low, levels_high)], recv_high.at[it, apart],
                part_s.at[it, 1], part_r.at[it, 1], peers[apart],
            )
        for apart in range(1, size_gy):
            send(
                send_part.at[it, apart.bit_length() - 1], recv_low.at[it, apart],
                part_s.at[it, 0], part_r.at[it, 0], peers[apart],
            )

    def others(ref, it):
        return ref.at[it, pl.ds(1, ref.shape[1] - 1)]

    def send_nodes(it):
        with phase(f"wait_parts{it}"):
            landed(others(recv_high, it), part_r.at[it, 1])
        total = send_part[it, levels_low:num_levels]
        for apart in range(1, size_gy):
            total = total + recv_high[it, apart]
        send_node[it] = total
        for apart in range(1, size_gx):
            send(
                send_node.at[it, apart.bit_length() - 1], recv_node.at[it, apart],
                node_s.at[it], node_r.at[it], peers[apart * size_gy],
            )

    def siblings(it):
        with phase(f"wait_nodes{it}"):
            landed(others(recv_low, it), part_r.at[it, 0])
            landed(others(recv_node, it), node_r.at[it])
        tiles = []
        for count, source in ((levels_low, recv_low), (levels_high, recv_node)):
            for level in range(count):
                total = source[it, 2**level]
                for apart in range(2**level + 1, 2 ** (level + 1)):
                    total = total + source[it, apart]
                tiles.append(total)
        if len(tiles) % 2:
            tiles.append(jnp.zeros_like(tiles[0]))
        blocks = []
        for pair in range(len(tiles) // 2):
            even, odd = tiles[2 * pair], tiles[2 * pair + 1]
            top = jnp.where(left_side, even, swap(odd))
            bottom = jnp.where(left_side, swap(even), odd)
            blocks.append(jnp.concatenate([top, bottom], axis=0))
        return jnp.concatenate(blocks, axis=1)

    slots = lanes // nv
    row16 = lax.broadcasted_iota(jnp.int32, (nv, lanes), 0)
    slot16 = lax.broadcasted_iota(jnp.int32, (nv, lanes), 1) - row16 * slots

    def send_sums(it, values):
        block = jnp.zeros((nv, lanes), f32)
        for idx, value in enumerate(values):
            block = jnp.where(slot16 == idx, value, block)
        send_dots[it] = jnp.sum(block, axis=0, keepdims=True)
        for apart in range(1, size_all):
            send(
                send_dots.at[it], recv_dots.at[it, apart],
                dots_s.at[it], dots_r.at[it], peers[apart],
            )

    def read_sums(it, count):
        with phase(f"wait_sums{it}"):
            landed(others(recv_dots, it), dots_r.at[it])
        terms = [send_dots[it]] + [recv_dots[it, apart] for apart in range(1, size_all)]
        while len(terms) > 1:
            terms = [terms[i] + terms[i + 1] for i in range(0, len(terms), 2)]
        return [
            jnp.sum(jnp.where(slot16 == idx, terms[0], 0.0), axis=1, keepdims=True)
            for idx in range(count)
        ]

    chunk = min(256, leaf_len)

    def near_columns(both, first, begin, end):
        for low in range(begin, end, chunk):
            high = low + chunk
            cols = slice(low, high)
            wide = dot(both[:, :high], near_hi[:high, cols])
            rest = dot(first[:, :high], near_lo[:high, cols])
            if high < leaf_len:
                wide = wide + dot(both[:, high:], near_hi[cols, high:], NT)
                rest = rest + dot(first[:, high:], near_lo[cols, high:], NT)
            image_ref[:, cols] = wide[:nv] + wide[nv:] + rest

    strip = min(128, chunk)

    def fill_near(both, first, begin, end):
        for low in range(begin, end, chunk):
            high = low + chunk
            cols = slice(low, high)
            for base in range(0, high, strip):
                rows = slice(base, base + strip)
                square = dot(left_ref[rows, :], right_ref[:, cols])
                square = jnp.maximum(square, 1e-30)
                distance = square * lax.rsqrt(square)
                value = (1.0 + distance) * jnp.exp2(distance * (-log2_e))
                hi, lo = split2(value)
                near_hi[rows, cols] = hi
                near_lo[rows, cols] = lo
            wide = dot(both[:, :high], near_hi[:high, cols])
            image_ref[:, cols] = wide[:nv] + wide[nv:] + dot(first[:, :high], near_lo[:high, cols])
            if low:
                wide = dot(both[:, cols], near_hi[:low, cols], NT)
                rest = dot(first[:, cols], near_lo[:low, cols], NT)
                image_ref[:, :low] += wide[:nv] + wide[nv:] + rest

    def prepare_points():
        with phase("gather_pos"):
            coords = jnp.concatenate([coords_ref[...], jnp.zeros((16 - num_dims, leaf_len), f32)], axis=0)
            gathered = gather(jnp.concatenate(split3(coords), axis=0), 3)[:8]
        row8 = lax.broadcasted_iota(jnp.int32, (8, 1), 0)
        with phase("place"):
            scale = jnp.zeros((8, 1), f32)
            for dim in range(num_dims):
                scale = jnp.where(row8 == dim, inv_ref[dim] * sqrt_three, scale)
            place = (gathered - 0.5) * scale
            coarse = jnp.round(place * 4.0) * 0.25
            fine_hi, fine_lo = split2(place - coarse)
            fine_hi, fine_lo = fine_hi.astype(f32), fine_lo.astype(f32)
            fine = fine_hi + fine_lo
            whole_norm = jnp.sum(coarse * coarse, axis=0, keepdims=True)
            rest_norm = jnp.sum(fine * (2.0 * coarse + fine), axis=0, keepdims=True)
        def rows_of(values):
            block = jnp.zeros((8, leaf_len), f32)
            for idx, value in enumerate(values):
                block = jnp.where(row8 == idx, value, block)
            return block

        with phase("lr"):
            norms = [part.astype(f32) for part in split2(whole_norm)]
            rests = [part.astype(f32) for part in split3(rest_norm)]
            ones = [1.0] * 3
            pairs = [
                (-2.0 * coarse, coarse),
                (rows_of(norms + ones[:2]), rows_of(ones[:2] + norms)),
                (rows_of(rests + ones), rows_of(ones + rests)),
                (-2.0 * coarse, fine_hi),
                (-2.0 * coarse, fine_lo),
                (fine_hi, -2.0 * coarse),
                (fine_lo, -2.0 * coarse),
                (fine_hi, -2.0 * fine_hi),
                (fine_hi, -2.0 * fine_lo),
                (fine_lo, -2.0 * fine_hi),
            ]
            blank = jnp.zeros((128 - 8 * len(pairs), leaf_len), f32)
            left_ref[...] = jnp.concatenate([pair[0] for pair in pairs] + [blank], axis=0).T.astype(bf16)
            right_ref[...] = jnp.concatenate([pair[1] for pair in pairs] + [blank], axis=0).astype(bf16)

    def operate(it, vector, meanwhile):
        first, second = split2(vector)
        both = jnp.concatenate([first, second], axis=0)
        if it == 0:
            with phase("wait_v"):
                v_load.wait()
            with phase("prep_v"):
                prepare(v_raw, v_hi, v_lo)
        with phase(f"coef{it}"):
            wide = dot(both, v_hi[...], NT)
            coef = wide[:nv] + wide[nv:] + dot(first, v_lo[...], NT)
        if it == 0:
            with phase("wait_barrier"):
                pl.semaphore_wait(barrier, size_all - 1)
        with phase(f"send_partials{it}"):
            send_partials(it, coef)
        meanwhile()
        if it == 0:
            with phase("fillA"):
                fill_near(both, first, 0, leaf_len * 3 // 4)
            send_nodes(it)
            with phase("fillB"):
                fill_near(both, first, leaf_len * 3 // 4, leaf_len)
            u_load.wait()
            with phase("prep_u"):
                prepare(u_raw, u_hi, u_lo)
        else:
            with phase(f"nearA{it}"):
                near_columns(both, first, 0, leaf_len // 2)
            send_nodes(it)
            with phase(f"nearB{it}"):
                near_columns(both, first, leaf_len // 2, leaf_len)
        coef_hi, coef_lo = split2(siblings(it))
        with phase(f"far{it}"):
            wide = dot(jnp.concatenate([coef_hi, coef_lo], axis=0), u_hi[...])
            far = wide[:nv] + wide[nv:] + dot(coef_hi, u_lo[...])
        return live * (image_ref[...] + far) - vector

    def lane_sum(value):
        return jnp.sum(value, axis=1, keepdims=True)

    shift = 1.0 + noise_ref[0]
    gram = {}
    columns = []
    images = []
    beta = None
    raw = basis_ref[0]
    image = operate(0, raw, prepare_points)
    for it in range(ITERS):
        last = it + 1 == ITERS
        def exchange_sums(it=it, raw=raw, image=image, last=last):
            with phase(f"sums{it}"):
                values = [lane_sum(basis_ref[row] * image) for row in range(it)] + [lane_sum(raw * image)]
                values += [lane_sum(basis_ref[row] * raw) for row in range(it)] + [lane_sum(raw * raw)]
                if last:
                    values.append(lane_sum(image * image))
                send_sums(it, values)

        if last:
            exchange_sums()
        else:
            ahead = operate(it + 1, image, exchange_sums)
        sums = read_sums(it, 2 * it + 2 + last)
        with phase(f"ortho{it}"):
            length = jnp.sqrt(sums[2 * it + 1] + epsilon)
            inverse = 1.0 / length
            if it == 0:
                beta = length
            else:
                columns[-1].append(length)
            products = [value * inverse for value in sums[: it + 1]]
            products[it] = products[it] * inverse
            lengths = [value * inverse for value in sums[it + 1 : 2 * it + 2]]
            lengths[it] = lengths[it] * inverse
            vector = raw * inverse
            basis_ref[it] = vector
            for row in range(it + 1):
                gram[row, it] = gram[it, row] = lengths[row]
            column = [products[row] + shift * lengths[row] for row in range(it + 1)]
            moved = [column[row] - shift if row == it else column[row] for row in range(it + 1)]
            columns.append(list(column))
            if last:
                rest = sums[-1] * inverse * inverse
                for row in range(it + 1):
                    inside = -2.0 * products[row]
                    for other in range(it + 1):
                        inside = inside + moved[other] * gram[row, other]
                    rest = rest + moved[row] * inside
                columns[-1].append(jnp.sqrt(jnp.maximum(rest, 0.0) + epsilon))
            else:
                images.append(image * inverse)
                raw = images[it]
                image = ahead * inverse
                for row in range(it + 1):
                    raw = raw - moved[row] * basis_ref[row]
                    image = image - moved[row] * images[row]
    with phase("solve"):
        weights = least_squares(columns, beta)
        solved = weights[0] * basis_ref[0]
        for it in range(1, ITERS):
            solved = solved + weights[it] * basis_ref[it]
    with phase("scatter"):
        parts = jnp.concatenate(split3(solved), axis=0)
        stacked = jnp.concatenate(
            [parts * jnp.where(outer == g, 1.0, 0.0).astype(bf16) for g in range(groups)], axis=0
        )
        got = dot(stacked, pick_ref[...], NT)
        for g in range(groups):
            base = g * 3 * nv
            out_ref[:, g * width : (g + 1) * width] = (
                got[base : base + nv] + got[base + nv : base + 2 * nv] + got[base + 2 * nv : base + 3 * nv]
            )
    for it in range(ITERS):
        landed(others(recv_high, it), part_s.at[it, 1])
        landed(others(recv_low, it), part_s.at[it, 0])
        landed(others(recv_node, it), node_s.at[it])
        landed(others(recv_dots, it), dots_s.at[it])


def per_device(
    size_gx, size_gy,
    coordinates, rhs, leaf_order, leaf_sizes, inverse_scales, noise_var, u_factors, v_factors,
):
    num_vectors, leaf_len = rhs.shape
    num_levels, num_rank = u_factors.shape[0], u_factors.shape[1]
    levels_high = size_gx.bit_length() - 1
    half, lanes = num_vectors // 2, 2 * num_rank
    padded = (num_levels + 1) // 2 * 2 * num_rank
    tile = (half, lanes)
    vmem = pl.BlockSpec(memory_space=pltpu.VMEM)
    smem = pl.BlockSpec(memory_space=pltpu.SMEM)
    any_space = pl.BlockSpec(memory_space=pl.ANY)
    dma = pltpu.SemaphoreType.DMA
    return pl.pallas_call(
        functools.partial(fused, size_gx, size_gy),
        out_shape=jax.ShapeDtypeStruct(rhs.shape, f32),
        in_specs=[vmem, vmem, vmem, smem, smem, smem, any_space, any_space],
        out_specs=vmem,
        scratch_shapes=[
            pltpu.VMEM((leaf_len, leaf_len), bf16),
            pltpu.VMEM((leaf_len, leaf_len), bf16),
            pltpu.VMEM((256, leaf_len), bf16),
            pltpu.VMEM((leaf_len, 128), bf16),
            pltpu.VMEM((128, leaf_len), bf16),
            pltpu.VMEM(u_factors.shape, f32),
            pltpu.VMEM(v_factors.shape, f32),
            pltpu.VMEM((padded, leaf_len), bf16),
            pltpu.VMEM((padded, leaf_len), bf16),
            pltpu.VMEM((padded, leaf_len), bf16),
            pltpu.VMEM((padded, leaf_len), bf16),
            pltpu.VMEM((ITERS,) + rhs.shape, f32),
            pltpu.VMEM(rhs.shape, f32),
            pltpu.VMEM((ITERS, num_levels) + tile, f32),
            pltpu.VMEM((ITERS, size_gy) + tile, f32),
            pltpu.VMEM((ITERS, size_gy, levels_high) + tile, f32),
            pltpu.VMEM((ITERS, levels_high) + tile, f32),
            pltpu.VMEM((ITERS, size_gx) + tile, f32),
            pltpu.VMEM((ITERS, 1, lanes), f32),
            pltpu.VMEM((ITERS, size_gx * size_gy, 1, lanes), f32),
            dma((2,)),
            dma((ITERS, 2)),
            dma((ITERS, 2)),
            dma((ITERS,)),
            dma((ITERS,)),
            dma((ITERS,)),
            dma((ITERS,)),
        ],
        compiler_params=pltpu.CompilerParams(collective_id=0, has_side_effects=True),
        name="gmres",
    )(coordinates, rhs, leaf_order, leaf_sizes, inverse_scales, noise_var, u_factors, v_factors)


def solution(mesh):
    in_specs = (
        P(None, ("gx", "gy")),
        P(None, ("gx", "gy")),
        P(("gx", "gy"), None),
        P(("gx", "gy")),
        P(),
        P(),
        P(None, None, ("gx", "gy")),
        P(None, None, ("gx", "gy")),
    )
    out_specs = P(None, ("gx", "gy"))
    return jax.shard_map(
        functools.partial(per_device, mesh.shape["gx"], mesh.shape["gy"]),
        mesh=mesh, in_specs=in_specs, out_specs=out_specs, check_vma=False,
    )
```

time: 53.1 us -> 45.8 us (0.86)
  Pallas kernels: 50.1 us -> 42.7 us
    pallas_call x1, Pallas kernels: 50.1 us -> 42.7 us  [per_device(): pl.pallas_call(functools.partial(fused, size_gx, size_gy), out_shape=jax....]
where the time goes in v1:
time: 45.8 us; the launch traced here: 45.6 us
  Pallas kernels  42.7 us (93%)
  local copies, waits for them, and re-layouts  1.57 us (3%)
  between operations  1.31 us (3%)
    pallas_call x1, Pallas kernels, per_device(): pl.pallas_call(functools.partial(fused, size_gx, size_gy), out_shape=jax....  42.7 us
    unnamed x1, local copies, waits for them, and re-layouts  1.57 us

profile of v1, /device:TPU:0, one launch (start us, length us, event | category | flops | bytes accessed | tf_op | source)
XLA Modules:
  0.0 45.6 jit_solution(18307306246663427261)
XLA Ops:
  1.3 42.7 %gmres.1 = f32[16,2048]{1,0:T(8,128)} custom-call(f32[3,2048]{1,0:T(4,128)} %coords_ref.1, f32[16,2048]{1,0:T(8,128)} %rhs_ref.1, s32[1,2048]{1,0:T(1,128)} %order_ref.1, s32[1]{0:T(128)S(6)} %copy.10.sizes_ref, f32[3]{0:T(128)} %inv_ref.1, f32[1]{0:T(128)S(6)} %copy.11.noise_ref, f32[5,64,2048]{2,1,0:T(8,128)} %u_hbm.1, f32[5,64,2048]{2,1,0:T(8,128)} %v_hbm.1), custom_call_target="tpu_custom_call" | custom-call | tf_op jit(solution)/shard_map/gmres/pallas_call | solution.py:480
  44.1 1.6 %copy.12 = f32[16,2048]{1,0:T(8,128)} copy(f32[16,2048]{1,0:T(8,128)} %gmres.1) | data formatting | bytes 262144

commit v2 on v1

--- a/solution.py
+++ b/solution.py
@@ -91,9 +91,10 @@
 
 def fused(
     size_gx, size_gy,
-    coords_ref, rhs_ref, order_ref, sizes_ref, inv_ref, noise_ref, u_hbm, v_hbm,
+    coords_hbm, rhs_hbm, order_hbm, sizes_hbm, inv_hbm, noise_hbm, u_hbm, v_hbm,
     out_ref,
-    near_hi, near_lo, pick_ref, left_ref, right_ref, u_raw, v_raw, u_hi, u_lo, v_hi, v_lo,
+    coords_ref, rhs_ref, order_ref, sizes_ref, inv_ref, noise_ref,
+    near_hi, near_lo, pick_ref, left_ref, right_ref, u_raw, v_raw, u_all, v_all, vt_all, mix_all,
     basis_ref, image_ref,
     send_part, recv_low, recv_high, send_node, recv_node,
     send_dots, recv_dots,
@@ -111,10 +112,16 @@
     lanes = 2 * num_rank
     size_all = size_gx * size_gy
 
-    u_load = pltpu.make_async_copy(u_hbm, u_raw, load_sem.at[0])
-    v_load = pltpu.make_async_copy(v_hbm, v_raw, load_sem.at[1])
-    v_load.start()
-    u_load.start()
+    loads = [
+        pltpu.make_async_copy(src, dst, load_sem.at[idx])
+        for idx, (src, dst) in enumerate((
+            (order_hbm, order_ref), (rhs_hbm, rhs_ref), (sizes_hbm, sizes_ref), (v_hbm, v_raw),
+            (coords_hbm, coords_ref), (inv_hbm, inv_ref), (noise_hbm, noise_ref), (u_hbm, u_raw),
+        ))
+    ]
+    for load in loads:
+        load.start()
+    v_load, u_load = loads[3], loads[7]
 
     peers = [
         (flipped(me_x, apart // size_gy), flipped(me_y, apart % size_gy)) for apart in range(size_all)
@@ -133,6 +140,8 @@
     def landed(block, sem):
         pltpu.make_async_copy(block, block, sem).wait()
 
+    for load in loads[:3]:
+        load.wait()
     live = jnp.where(
         lax.broadcasted_iota(jnp.int32, (1, leaf_len), 1) < sizes_ref[0], 1.0, 0.0
     ).astype(f32)
@@ -150,10 +159,10 @@
         rows = stack.shape[0] // pieces
         stacked = jnp.concatenate([stack[:, g * width : (g + 1) * width] for g in range(groups)], axis=0)
         blocks = []
-        for start_col in range(0, leaf_len, 512):
-            cols = slice(start_col, start_col + 512)
+        for start_col in range(0, leaf_len, width):
+            cols = slice(start_col, start_col + width)
             got = dot(stacked, pick_ref[:, cols])
-            total = jnp.zeros((rows, 512), f32)
+            total = jnp.zeros((rows, width), f32)
             for g in range(groups):
                 term = None
                 for piece in range(pieces):
@@ -164,19 +173,20 @@
         return jnp.concatenate(blocks, axis=1)
 
     with phase("gather_rhs"):
-        basis_ref[0] = live * gather(jnp.concatenate(split3(rhs_ref[...]), axis=0), 3)
-
-    padded = v_hi.shape[0]
+        basis_ref[0] = live * gather(jnp.concatenate(split2(rhs_ref[...]), axis=0), 2)
+
+    padded = v_all.shape[0] // 2
     used = num_levels * num_rank
 
-    def prepare(raw, hi, lo):
+    def prepare(raw, both, mask=None):
         for level in range(num_levels):
-            first, second = split2(raw[level])
-            hi[level * num_rank : (level + 1) * num_rank, :] = first
-            lo[level * num_rank : (level + 1) * num_rank, :] = second
+            first, second = split2(raw[level] if mask is None else raw[level] * mask)
+            low = level * num_rank
+            both[low : low + num_rank, :] = first
+            both[padded + low : padded + low + num_rank, :] = second
         if padded > used:
-            hi[used:, :] = jnp.zeros((padded - used, leaf_len), bf16)
-            lo[used:, :] = jnp.zeros((padded - used, leaf_len), bf16)
+            both[used:padded, :] = jnp.zeros((padded - used, leaf_len), bf16)
+            both[padded + used :, :] = jnp.zeros((padded - used, leaf_len), bf16)
 
     lane = lax.broadcasted_iota(jnp.int32, (half, lanes), 1)
     left_side = lane < num_rank
@@ -269,40 +279,66 @@
 
     chunk = min(256, leaf_len)
 
+    def doubled(value):
+        first, second = split2(value)
+        return jnp.concatenate([first, second], axis=0), first
+
+    def product(both, first, hi, lo, dims=NN):
+        wide = dot(both, hi, dims)
+        return wide[:nv] + wide[nv:] + dot(first, lo, dims)
+
     def near_columns(both, first, begin, end):
         for low in range(begin, end, chunk):
             high = low + chunk
             cols = slice(low, high)
-            wide = dot(both[:, :high], near_hi[:high, cols])
-            rest = dot(first[:, :high], near_lo[:high, cols])
+            total = product(both[:, :high], first[:, :high], near_hi[:high, cols], near_lo[:high, cols])
             if high < leaf_len:
-                wide = wide + dot(both[:, high:], near_hi[cols, high:], NT)
-                rest = rest + dot(first[:, high:], near_lo[cols, high:], NT)
-            image_ref[:, cols] = wide[:nv] + wide[nv:] + rest
+                total = total + product(
+                    both[:, high:], first[:, high:], near_hi[cols, high:], near_lo[cols, high:], NT
+                )
+            image_ref[:, cols] = total
 
     strip = min(128, chunk)
 
+    def fill_tile(low, base):
+        cols = slice(low, low + chunk)
+        for start in range(base, base + chunk, strip):
+            rows = slice(start, start + strip)
+            square = jnp.maximum(dot(left_ref[rows, :], right_ref[:, cols]), 1e-30)
+            distance = square * lax.rsqrt(square)
+            value = (1.0 + distance) * jnp.exp2(distance * (-log2_e))
+            hi, lo = split2(value)
+            near_hi[rows, cols] = hi
+            near_lo[rows, cols] = lo
+
+    def near_tile(both, first, low, base):
+        cols, rows = slice(low, low + chunk), slice(base, base + chunk)
+        part = product(both[:, rows], first[:, rows], near_hi[rows, cols], near_lo[rows, cols])
+        if base:
+            image_ref[:, cols] += part
+        else:
+            image_ref[:, cols] = part
+        if base < low:
+            image_ref[:, rows] += product(
+                both[:, cols], first[:, cols], near_hi[rows, cols], near_lo[rows, cols], NT
+            )
+
+    tiles_all = [(low, base) for low in range(0, leaf_len, chunk) for base in range(0, low + chunk, chunk)]
+
     def fill_near(both, first, begin, end):
-        for low in range(begin, end, chunk):
-            high = low + chunk
-            cols = slice(low, high)
-            for base in range(0, high, strip):
-                rows = slice(base, base + strip)
-                square = dot(left_ref[rows, :], right_ref[:, cols])
-                square = jnp.maximum(square, 1e-30)
-                distance = square * lax.rsqrt(square)
-                value = (1.0 + distance) * jnp.exp2(distance * (-log2_e))
-                hi, lo = split2(value)
-                near_hi[rows, cols] = hi
-                near_lo[rows, cols] = lo
-            wide = dot(both[:, :high], near_hi[:high, cols])
-            image_ref[:, cols] = wide[:nv] + wide[nv:] + dot(first[:, :high], near_lo[:high, cols])
-            if low:
-                wide = dot(both[:, cols], near_hi[:low, cols], NT)
-                rest = dot(first[:, cols], near_lo[:low, cols], NT)
-                image_ref[:, :low] += wide[:nv] + wide[nv:] + rest
+        for idx in range(begin, end):
+            low, base = tiles_all[idx]
+            fill_tile(low, base)
+            if base == low:
+                cols = slice(low, low + chunk)
+                vt_all[cols, :] = v_all[:, cols].T
+            if idx > begin:
+                near_tile(both, first, *tiles_all[idx - 1])
+        near_tile(both, first, *tiles_all[end - 1])
 
     def prepare_points():
+        for load in loads[4:7]:
+            load.wait()
         with phase("gather_pos"):
             coords = jnp.concatenate([coords_ref[...], jnp.zeros((16 - num_dims, leaf_len), f32)], axis=0)
             gathered = gather(jnp.concatenate(split3(coords), axis=0), 3)[:8]
@@ -344,70 +380,104 @@
             left_ref[...] = jnp.concatenate([pair[0] for pair in pairs] + [blank], axis=0).T.astype(bf16)
             right_ref[...] = jnp.concatenate([pair[1] for pair in pairs] + [blank], axis=0).astype(bf16)
 
-    def operate(it, vector, meanwhile):
-        first, second = split2(vector)
-        both = jnp.concatenate([first, second], axis=0)
-        if it == 0:
-            with phase("wait_v"):
-                v_load.wait()
-            with phase("prep_v"):
-                prepare(v_raw, v_hi, v_lo)
-        with phase(f"coef{it}"):
-            wide = dot(both, v_hi[...], NT)
-            coef = wide[:nv] + wide[nv:] + dot(first, v_lo[...], NT)
-        if it == 0:
-            with phase("wait_barrier"):
-                pl.semaphore_wait(barrier, size_all - 1)
+    def against(both, factors, dims=NN):
+        size = factors.shape[0 if dims == NT else 1] // 2
+        wide = dot(both, factors[...], dims)
+        return wide[:nv, :size] + wide[nv:, :size] + wide[:nv, size:]
+
+    def coefs_of(name, value):
+        with phase(f"coefs_{name}"):
+            return against(doubled(value)[0], vt_all)
+
+    def far_of(it, coef):
+        with phase(f"far{it}"):
+            first, second = split2(coef)
+            left = jnp.concatenate(
+                [
+                    jnp.concatenate([first, first], axis=1),
+                    jnp.concatenate([second, jnp.zeros_like(second)], axis=1),
+                ],
+                axis=0,
+            )
+            wide = dot(left, u_all[...])
+            return wide[:nv] + wide[nv:]
+
+    def start_exchange(it, coef):
         with phase(f"send_partials{it}"):
             send_partials(it, coef)
-        meanwhile()
-        if it == 0:
-            with phase("fillA"):
-                fill_near(both, first, 0, leaf_len * 3 // 4)
-            send_nodes(it)
-            with phase("fillB"):
-                fill_near(both, first, leaf_len * 3 // 4, leaf_len)
-            u_load.wait()
-            with phase("prep_u"):
-                prepare(u_raw, u_hi, u_lo)
-        else:
-            with phase(f"nearA{it}"):
-                near_columns(both, first, 0, leaf_len // 2)
-            send_nodes(it)
-            with phase(f"nearB{it}"):
-                near_columns(both, first, leaf_len // 2, leaf_len)
-        coef_hi, coef_lo = split2(siblings(it))
-        with phase(f"far{it}"):
-            wide = dot(jnp.concatenate([coef_hi, coef_lo], axis=0), u_hi[...])
-            far = wide[:nv] + wide[nv:] + dot(coef_hi, u_lo[...])
-        return live * (image_ref[...] + far) - vector
+
+    def operate_first(vector):
+        both, first = doubled(vector)
+        with phase("wait_v"):
+            v_load.wait()
+        with phase("prep_v"):
+            prepare(v_raw, v_all)
+        with phase("coef0"):
+            coef = against(both, v_all, NT)
+        with phase("wait_barrier"):
+            pl.semaphore_wait(barrier, size_all - 1)
+        start_exchange(0, coef)
+        prepare_points()
+        with phase("fillA"):
+            fill_near(both, first, 0, len(tiles_all) * 5 // 9)
+        send_nodes(0)
+        with phase("fillB"):
+            fill_near(both, first, len(tiles_all) * 5 // 9, len(tiles_all))
+        u_load.wait()
+        with phase("prep_u"):
+            prepare(u_raw, u_all, live)
+        return live * image_ref[...] - vector + far_of(0, siblings(0))
+
+    def operate_near(it, vector, relay):
+        both, first = doubled(vector)
+        with phase(f"nearA{it}"):
+            near_columns(both, first, 0, relay)
+        send_nodes(it)
+        with phase(f"nearB{it}"):
+            near_columns(both, first, relay, leaf_len)
+        return live * image_ref[...] - vector
+
+    def prepare_mix():
+        with phase("mix"):
+            wide = dot(u_all[:used, :], vt_all[...])
+            mix = wide[:, :padded] + wide[:, padded:] + dot(u_all[padded : padded + used, :], vt_all[:, :padded])
+            first, second = split2(mix)
+            mix_all[:used, :padded] = first
+            mix_all[:used, padded:] = second
+            if padded > used:
+                mix_all[used:, :] = jnp.zeros((padded - used, 2 * padded), bf16)
 
     def lane_sum(value):
         return jnp.sum(value, axis=1, keepdims=True)
 
-    shift = 1.0 + noise_ref[0]
     gram = {}
     columns = []
     images = []
     beta = None
     raw = basis_ref[0]
-    image = operate(0, raw, prepare_points)
+    image = operate_first(raw)
+    shift = 1.0 + noise_ref[0]
+    coef = coefs_of("first", image)
+    coefs = []
+    start_exchange(1, coef)
     for it in range(ITERS):
         last = it + 1 == ITERS
-        def exchange_sums(it=it, raw=raw, image=image, last=last):
-            with phase(f"sums{it}"):
-                values = [lane_sum(basis_ref[row] * image) for row in range(it)] + [lane_sum(raw * image)]
-                values += [lane_sum(basis_ref[row] * raw) for row in range(it)] + [lane_sum(raw * raw)]
-                if last:
-                    values.append(lane_sum(image * image))
-                send_sums(it, values)
-
-        if last:
-            exchange_sums()
-        else:
-            ahead = operate(it + 1, image, exchange_sums)
-        sums = read_sums(it, 2 * it + 2 + last)
-        with phase(f"ortho{it}"):
+        ahead = it + 2 < ITERS
+        with phase(f"sums{it}"):
+            values = [lane_sum(basis_ref[row] * image) for row in range(it)] + [lane_sum(raw * image)]
+            values += [lane_sum(basis_ref[row] * raw) for row in range(it)] + [lane_sum(raw * raw)]
+            if last:
+                values.append(lane_sum(image * image))
+            send_sums(it, values)
+        if not last:
+            near = operate_near(it + 1, image, leaf_len * (7 if it == 0 else 6) // 8)
+            if ahead:
+                near_coef = coefs_of(f"near{it}", near)
+                if it == 0:
+                    prepare_mix()
+            found = siblings(it + 1)
+        sums = read_sums(it, len(values))
+        with phase(f"scalars{it}"):
             length = jnp.sqrt(sums[2 * it + 1] + epsilon)
             inverse = 1.0 / length
             if it == 0:
@@ -418,13 +488,23 @@
             products[it] = products[it] * inverse
             lengths = [value * inverse for value in sums[it + 1 : 2 * it + 2]]
             lengths[it] = lengths[it] * inverse
-            vector = raw * inverse
-            basis_ref[it] = vector
             for row in range(it + 1):
                 gram[row, it] = gram[it, row] = lengths[row]
             column = [products[row] + shift * lengths[row] for row in range(it + 1)]
             moved = [column[row] - shift if row == it else column[row] for row in range(it + 1)]
             columns.append(list(column))
+        if ahead:
+            with phase(f"coefs_next{it}"):
+                coefs.append(coef * inverse)
+                coef = (near_coef + against(doubled(found)[0], mix_all)) * inverse
+                for row in range(it + 1):
+                    coef = coef - moved[row] * coefs[row]
+            start_exchange(it + 2, coef)
+        if not last:
+            following = near + far_of(it + 1, found)
+        with phase(f"ortho{it}"):
+            vector = raw * inverse
+            basis_ref[it] = vector
             if last:
                 rest = sums[-1] * inverse * inverse
                 for row in range(it + 1):
@@ -436,7 +516,7 @@
             else:
                 images.append(image * inverse)
                 raw = images[it]
-                image = ahead * inverse
+                image = following * inverse
                 for row in range(it + 1):
                     raw = raw - moved[row] * basis_ref[row]
                     image = image - moved[row] * images[row]
@@ -446,16 +526,14 @@
         for it in range(1, ITERS):
             solved = solved + weights[it] * basis_ref[it]
     with phase("scatter"):
-        parts = jnp.concatenate(split3(solved), axis=0)
+        parts = jnp.concatenate(split2(solved), axis=0)
         stacked = jnp.concatenate(
             [parts * jnp.where(outer == g, 1.0, 0.0).astype(bf16) for g in range(groups)], axis=0
         )
         got = dot(stacked, pick_ref[...], NT)
         for g in range(groups):
-            base = g * 3 * nv
-            out_ref[:, g * width : (g + 1) * width] = (
-                got[base : base + nv] + got[base + nv : base + 2 * nv] + got[base + 2 * nv : base + 3 * nv]
-            )
+            base = 2 * g * nv
+            out_ref[:, g * width : (g + 1) * width] = got[base : base + nv] + got[base + nv : base + 2 * nv]
     for it in range(ITERS):
         landed(others(recv_high, it), part_s.at[it, 1])
         landed(others(recv_low, it), part_s.at[it, 0])
@@ -474,15 +552,20 @@
     padded = (num_levels + 1) // 2 * 2 * num_rank
     tile = (half, lanes)
     vmem = pl.BlockSpec(memory_space=pltpu.VMEM)
-    smem = pl.BlockSpec(memory_space=pltpu.SMEM)
-    any_space = pl.BlockSpec(memory_space=pl.ANY)
+    hbm = pl.BlockSpec(memory_space=pltpu.HBM)
     dma = pltpu.SemaphoreType.DMA
     return pl.pallas_call(
         functools.partial(fused, size_gx, size_gy),
         out_shape=jax.ShapeDtypeStruct(rhs.shape, f32),
-        in_specs=[vmem, vmem, vmem, smem, smem, smem, any_space, any_space],
+        in_specs=[hbm] * 8,
         out_specs=vmem,
         scratch_shapes=[
+            pltpu.VMEM(coordinates.shape, f32),
+            pltpu.VMEM(rhs.shape, f32),
+            pltpu.VMEM(leaf_order.shape, jnp.int32),
+            pltpu.SMEM(leaf_sizes.shape, jnp.int32),
+            pltpu.SMEM(inverse_scales.shape, f32),
+            pltpu.SMEM(noise_var.shape, f32),
             pltpu.VMEM((leaf_len, leaf_len), bf16),
             pltpu.VMEM((leaf_len, leaf_len), bf16),
             pltpu.VMEM((256, leaf_len), bf16),
@@ -490,10 +573,10 @@
             pltpu.VMEM((128, leaf_len), bf16),
             pltpu.VMEM(u_factors.shape, f32),
             pltpu.VMEM(v_factors.shape, f32),
-            pltpu.VMEM((padded, leaf_len), bf16),
-            pltpu.VMEM((padded, leaf_len), bf16),
-            pltpu.VMEM((padded, leaf_len), bf16),
-            pltpu.VMEM((padded, leaf_len), bf16),
+            pltpu.VMEM((2 * padded, leaf_len), bf16),
+            pltpu.VMEM((2 * padded, leaf_len), bf16),
+            pltpu.VMEM((leaf_len, 2 * padded), bf16),
+            pltpu.VMEM((padded, 2 * padded), bf16),
             pltpu.VMEM((ITERS,) + rhs.shape, f32),
             pltpu.VMEM(rhs.shape, f32),
             pltpu.VMEM((ITERS, num_levels) + tile, f32),
@@ -503,7 +586,7 @@
             pltpu.VMEM((ITERS, size_gx) + tile, f32),
             pltpu.VMEM((ITERS, 1, lanes), f32),
             pltpu.VMEM((ITERS, size_gx * size_gy, 1, lanes), f32),
-            dma((2,)),
+            dma((8,)),
             dma((ITERS, 2)),
             dma((ITERS, 2)),
             dma((ITERS,)),

time: 45.8 us -> 42.5 us (0.928)
  Pallas kernels: 42.7 us -> 39.4 us
    pallas_call x1, Pallas kernels: 42.7 us -> 39.4 us  [per_device(): pl.pallas_call(functools.partial(fused, size_gx, size_gy), out_shape=jax....]
where the time goes in v2:
time: 42.5 us; the launch traced here: 42.3 us
  Pallas kernels  39.4 us (93%)
  local copies, waits for them, and re-layouts  1.57 us (4%)
  between operations  1.31 us (3%)
    pallas_call x1, Pallas kernels, per_device(): pl.pallas_call(functools.partial(fused, size_gx, size_gy), out_shape=jax....  39.4 us
    unnamed x1, local copies, waits for them, and re-layouts  1.57 us

profile of v2, /device:TPU:0, one launch (start us, length us, event | category | flops | bytes accessed | tf_op | source)
XLA Modules:
  0.0 42.3 jit_solution(1724870612180692876)
XLA Ops:
  1.3 39.4 %gmres.1 = f32[16,2048]{1,0:T(8,128)} custom-call(f32[3,2048]{1,0:T(4,128)} %coords_hbm.1, f32[16,2048]{1,0:T(8,128)} %rhs_hbm.1, s32[1,2048]{1,0:T(1,128)} %order_hbm.1, s32[1]{0:T(128)S(6)} %copy.10.sizes_hbm, f32[3]{0:T(128)} %inv_hbm.1, f32[1]{0:T(128)S(6)} %copy.11.noise_hbm, f32[5,64,2048]{2,1,0:T(8,128)} %u_hbm.1, f32[5,64,2048]{2,1,0:T(8,128)} %v_hbm.1), custom_call_target="tpu_custom_call" | custom-call | tf_op jit(solution)/shard_map/gmres/pallas_call | solution.py:557
  40.8 1.6 %copy.12 = f32[16,2048]{1,0:T(8,128)} copy(f32[16,2048]{1,0:T(8,128)} %gmres.1) | data formatting | bytes 262144

commit v3 on v2

--- a/solution.py
+++ b/solution.py
@@ -96,7 +96,7 @@
     coords_ref, rhs_ref, order_ref, sizes_ref, inv_ref, noise_ref,
     near_hi, near_lo, pick_ref, left_ref, right_ref, u_raw, v_raw, u_all, v_all, vt_all, mix_all,
     basis_ref, image_ref,
-    send_part, recv_low, recv_high, send_node, recv_node,
+    send_low, send_high, recv_low, recv_high, send_node, recv_node, spread_ref,
     send_dots, recv_dots,
     load_sem,
     part_s, part_r, node_s, node_r, dots_s, dots_r,
@@ -109,7 +109,9 @@
     num_dims = coords_ref.shape[0]
     num_levels, num_rank = u_raw.shape[0], u_raw.shape[1]
     half = nv // 2
+    quarter = nv // 4
     lanes = 2 * num_rank
+    my_core = lax.rem(me_y, 2)
     size_all = size_gx * size_gy
 
     loads = [
@@ -202,15 +204,19 @@
                 tile = jnp.where(left_side, top, swap(bottom))
             else:
                 tile = jnp.where(left_side, swap(top), bottom)
-            send_part[it, level] = tile
-        for apart in range(1, size_gy):
+            if level < levels_low:
+                send_low[it, level] = tile
+            else:
+                for part in range(2):
+                    send_high[it, part, level - levels_low] = tile[part * quarter : (part + 1) * quarter]
+        for apart in reversed(range(1, size_gy)):
             send(
-                send_part.at[it, pl.ds(levels_low, levels_high)], recv_high.at[it, apart],
+                send_high.at[it, lax.rem(peers[apart][1], 2)], recv_high.at[it, apart],
                 part_s.at[it, 1], part_r.at[it, 1], peers[apart],
             )
-        for apart in range(1, size_gy):
+        for apart in reversed(range(1, size_gy)):
             send(
-                send_part.at[it, apart.bit_length() - 1], recv_low.at[it, apart],
+                send_low.at[it, apart.bit_length() - 1], recv_low.at[it, apart],
                 part_s.at[it, 0], part_r.at[it, 0], peers[apart],
             )
 
@@ -220,15 +226,16 @@
     def send_nodes(it):
         with phase(f"wait_parts{it}"):
             landed(others(recv_high, it), part_r.at[it, 1])
-        total = send_part[it, levels_low:num_levels]
+        total = send_high[it, my_core]
         for apart in range(1, size_gy):
             total = total + recv_high[it, apart]
         send_node[it] = total
-        for apart in range(1, size_gx):
-            send(
-                send_node.at[it, apart.bit_length() - 1], recv_node.at[it, apart],
-                node_s.at[it], node_r.at[it], peers[apart * size_gy],
-            )
+        for apart in reversed(range(1, size_gx)):
+            for core in range(2):
+                send(
+                    send_node.at[it, apart.bit_length() - 1], recv_node.at[it, apart, my_core],
+                    node_s.at[it], node_r.at[it], peers[apart * size_gy + core],
+                )
 
     def siblings(it):
         with phase(f"wait_nodes{it}"):
@@ -240,6 +247,8 @@
                 total = source[it, 2**level]
                 for apart in range(2**level + 1, 2 ** (level + 1)):
                     total = total + source[it, apart]
+                if source is recv_node:
+                    total = jnp.concatenate([total[0], total[1]], axis=0)
                 tiles.append(total)
         if len(tiles) % 2:
             tiles.append(jnp.zeros_like(tiles[0]))
@@ -260,7 +269,7 @@
         for idx, value in enumerate(values):
             block = jnp.where(slot16 == idx, value, block)
         send_dots[it] = jnp.sum(block, axis=0, keepdims=True)
-        for apart in range(1, size_all):
+        for apart in reversed(range(1, size_all)):
             send(
                 send_dots.at[it], recv_dots.at[it, apart],
                 dots_s.at[it], dots_r.at[it], peers[apart],
@@ -298,7 +307,7 @@
                 )
             image_ref[:, cols] = total
 
-    strip = min(128, chunk)
+    strip = min(256, chunk)
 
     def fill_tile(low, base):
         cols = slice(low, low + chunk)
@@ -340,8 +349,11 @@
         for load in loads[4:7]:
             load.wait()
         with phase("gather_pos"):
-            coords = jnp.concatenate([coords_ref[...], jnp.zeros((16 - num_dims, leaf_len), f32)], axis=0)
-            gathered = gather(jnp.concatenate(split3(coords), axis=0), 3)[:8]
+            parts = [part.astype(f32) for part in split3(coords_ref[...])]
+            spare = jnp.zeros((16 - 3 * num_dims, leaf_len), f32)
+            got = gather(jnp.concatenate(parts + [spare], axis=0).astype(bf16), 1)
+            gathered = got[:num_dims] + got[num_dims : 2 * num_dims] + got[2 * num_dims : 3 * num_dims]
+            gathered = jnp.concatenate([gathered, jnp.zeros((8 - num_dims, leaf_len), f32)], axis=0)
         row8 = lax.broadcasted_iota(jnp.int32, (8, 1), 0)
         with phase("place"):
             scale = jnp.zeros((8, 1), f32)
@@ -380,14 +392,14 @@
             left_ref[...] = jnp.concatenate([pair[0] for pair in pairs] + [blank], axis=0).T.astype(bf16)
             right_ref[...] = jnp.concatenate([pair[1] for pair in pairs] + [blank], axis=0).astype(bf16)
 
-    def against(both, factors, dims=NN):
-        size = factors.shape[0 if dims == NT else 1] // 2
-        wide = dot(both, factors[...], dims)
+    def against(both, factors):
+        size = factors.shape[1] // 2
+        wide = dot(both, factors[...])
         return wide[:nv, :size] + wide[nv:, :size] + wide[:nv, size:]
 
     def coefs_of(name, value):
         with phase(f"coefs_{name}"):
-            return against(doubled(value)[0], vt_all)
+            return product(*doubled(value), vt_all[:, :padded], vt_all[:, padded:])
 
     def far_of(it, coef):
         with phase(f"far{it}"):
@@ -413,7 +425,7 @@
         with phase("prep_v"):
             prepare(v_raw, v_all)
         with phase("coef0"):
-            coef = against(both, v_all, NT)
+            coef = product(both, first, v_all[:padded, :], v_all[padded:, :], NT)
         with phase("wait_barrier"):
             pl.semaphore_wait(barrier, size_all - 1)
         start_exchange(0, coef)
@@ -454,6 +466,17 @@
     columns = []
     images = []
     beta = None
+    def spread(row, vector):
+        parts = jnp.concatenate(split2(vector), axis=0)
+        stacked = jnp.concatenate(
+            [parts * jnp.where(outer == g, 1.0, 0.0).astype(bf16) for g in range(groups)], axis=0
+        )
+        got = dot(stacked, pick_ref[...], NT)
+        for g in range(groups):
+            base = 2 * g * nv
+            spread_ref[row, :, g * width : (g + 1) * width] = got[base : base + nv] + got[base + nv : base + 2 * nv]
+
+    last_it = ITERS - 1
     raw = basis_ref[0]
     image = operate_first(raw)
     shift = 1.0 + noise_ref[0]
@@ -470,12 +493,15 @@
                 values.append(lane_sum(image * image))
             send_sums(it, values)
         if not last:
-            near = operate_near(it + 1, image, leaf_len * (7 if it == 0 else 6) // 8)
+            near = operate_near(it + 1, image, leaf_len * (6 if it == 0 else 4) // 8)
             if ahead:
                 near_coef = coefs_of(f"near{it}", near)
                 if it == 0:
                     prepare_mix()
-            found = siblings(it + 1)
+        else:
+            for row in range(ITERS):
+                with phase(f"spread{row}"):
+                    spread(row, raw if row == it else basis_ref[row])
         sums = read_sums(it, len(values))
         with phase(f"scalars{it}"):
             length = jnp.sqrt(sums[2 * it + 1] + epsilon)
@@ -493,6 +519,8 @@
             column = [products[row] + shift * lengths[row] for row in range(it + 1)]
             moved = [column[row] - shift if row == it else column[row] for row in range(it + 1)]
             columns.append(list(column))
+        if not last:
+            found = siblings(it + 1)
         if ahead:
             with phase(f"coefs_next{it}"):
                 coefs.append(coef * inverse)
@@ -522,18 +550,11 @@
                     image = image - moved[row] * images[row]
     with phase("solve"):
         weights = least_squares(columns, beta)
-        solved = weights[0] * basis_ref[0]
+        weights[last_it] = weights[last_it] * inverse
+        solved = weights[0] * spread_ref[0]
         for it in range(1, ITERS):
-            solved = solved + weights[it] * basis_ref[it]
-    with phase("scatter"):
-        parts = jnp.concatenate(split2(solved), axis=0)
-        stacked = jnp.concatenate(
-            [parts * jnp.where(outer == g, 1.0, 0.0).astype(bf16) for g in range(groups)], axis=0
-        )
-        got = dot(stacked, pick_ref[...], NT)
-        for g in range(groups):
-            base = 2 * g * nv
-            out_ref[:, g * width : (g + 1) * width] = got[base : base + nv] + got[base + nv : base + 2 * nv]
+            solved = solved + weights[it] * spread_ref[it]
+        out_ref[...] = solved
     for it in range(ITERS):
         landed(others(recv_high, it), part_s.at[it, 1])
         landed(others(recv_low, it), part_s.at[it, 0])
@@ -550,7 +571,8 @@
     levels_high = size_gx.bit_length() - 1
     half, lanes = num_vectors // 2, 2 * num_rank
     padded = (num_levels + 1) // 2 * 2 * num_rank
-    tile = (half, lanes)
+    tile, part = (half, lanes), (half // 2, lanes)
+    levels_low = size_gy.bit_length() - 1
     vmem = pl.BlockSpec(memory_space=pltpu.VMEM)
     hbm = pl.BlockSpec(memory_space=pltpu.HBM)
     dma = pltpu.SemaphoreType.DMA
@@ -579,11 +601,13 @@
             pltpu.VMEM((padded, 2 * padded), bf16),
             pltpu.VMEM((ITERS,) + rhs.shape, f32),
             pltpu.VMEM(rhs.shape, f32),
-            pltpu.VMEM((ITERS, num_levels) + tile, f32),
+            pltpu.VMEM((ITERS, levels_low) + tile, f32),
+            pltpu.VMEM((ITERS, 2, levels_high) + part, f32),
             pltpu.VMEM((ITERS, size_gy) + tile, f32),
-            pltpu.VMEM((ITERS, size_gy, levels_high) + tile, f32),
-            pltpu.VMEM((ITERS, levels_high) + tile, f32),
-            pltpu.VMEM((ITERS, size_gx) + tile, f32),
+            pltpu.VMEM((ITERS, size_gy, levels_high) + part, f32),
+            pltpu.VMEM((ITERS, levels_high) + part, f32),
+            pltpu.VMEM((ITERS, size_gx, 2) + part, f32),
+            pltpu.VMEM((ITERS,) + rhs.shape, f32),
             pltpu.VMEM((ITERS, 1, lanes), f32),
             pltpu.VMEM((ITERS, size_gx * size_gy, 1, lanes), f32),
             dma((8,)),

time: 42.5 us -> 40.1 us (0.944)
  Pallas kernels: 39.4 us -> 37.1 us
    pallas_call x1, Pallas kernels: 39.4 us -> 37.1 us  [per_device(): pl.pallas_call(functools.partial(fused, size_gx, size_gy), out_shape=jax....]
where the time goes in v3:
time: 40.1 us; the launch traced here: 39.9 us
  Pallas kernels  37.1 us (93%)
  local copies, waits for them, and re-layouts  1.57 us (4%)
  between operations  1.31 us (3%)
    pallas_call x1, Pallas kernels, per_device(): pl.pallas_call(functools.partial(fused, size_gx, size_gy), out_shape=jax....  37.1 us
    unnamed x1, local copies, waits for them, and re-layouts  1.57 us

profile of v3, /device:TPU:0, one launch (start us, length us, event | category | flops | bytes accessed | tf_op | source)
XLA Modules:
  0.0 39.9 jit_solution(4898244873523610396)
XLA Ops:
  1.3 37.1 %gmres.1 = f32[16,2048]{1,0:T(8,128)} custom-call(f32[3,2048]{1,0:T(4,128)} %coords_hbm.1, f32[16,2048]{1,0:T(8,128)} %rhs_hbm.1, s32[1,2048]{1,0:T(1,128)} %order_hbm.1, s32[1]{0:T(128)S(6)} %copy.10.sizes_hbm, f32[3]{0:T(128)} %inv_hbm.1, f32[1]{0:T(128)S(6)} %copy.11.noise_hbm, f32[5,64,2048]{2,1,0:T(8,128)} %u_hbm.1, f32[5,64,2048]{2,1,0:T(8,128)} %v_hbm.1), custom_call_target="tpu_custom_call" | custom-call | tf_op jit(solution)/shard_map/gmres/pallas_call | solution.py:579
  38.4 1.6 %copy.12 = f32[16,2048]{1,0:T(8,128)} copy(f32[16,2048]{1,0:T(8,128)} %gmres.1) | data formatting | bytes 262144

commit v4 on v3

--- a/solution.py
+++ b/solution.py
@@ -179,6 +179,7 @@
 
     padded = v_all.shape[0] // 2
     used = num_levels * num_rank
+    lead = 2 * nv
 
     def prepare(raw, both, mask=None):
         for level in range(num_levels):
@@ -411,7 +412,7 @@
                 ],
                 axis=0,
             )
-            wide = dot(left, u_all[...])
+            wide = dot(left, u_all[lead:, :])
             return wide[:nv] + wide[nv:]
 
     def start_exchange(it, coef):
@@ -437,7 +438,7 @@
             fill_near(both, first, len(tiles_all) * 5 // 9, len(tiles_all))
         u_load.wait()
         with phase("prep_u"):
-            prepare(u_raw, u_all, live)
+            prepare(u_raw, u_all.at[pl.ds(lead, 2 * padded)], live)
         return live * image_ref[...] - vector + far_of(0, siblings(0))
 
     def operate_near(it, vector, relay):
@@ -449,15 +450,18 @@
             near_columns(both, first, relay, leaf_len)
         return live * image_ref[...] - vector
 
-    def prepare_mix():
+    def prepare_mix(near):
         with phase("mix"):
-            wide = dot(u_all[:used, :], vt_all[...])
-            mix = wide[:, :padded] + wide[:, padded:] + dot(u_all[padded : padded + used, :], vt_all[:, :padded])
+            u_all[:lead, :] = doubled(near)[0]
+            wide = dot(u_all[: lead + used, :], vt_all[...])
+            begin = lead + padded
+            mix = wide[lead:, :padded] + wide[lead:, padded:] + dot(u_all[begin : begin + used, :], vt_all[:, :padded])
             first, second = split2(mix)
             mix_all[:used, :padded] = first
             mix_all[:used, padded:] = second
             if padded > used:
                 mix_all[used:, :] = jnp.zeros((padded - used, 2 * padded), bf16)
+            return wide[:nv, :padded] + wide[nv:lead, :padded] + wide[:nv, padded:]
 
     def lane_sum(value):
         return jnp.sum(value, axis=1, keepdims=True)
@@ -495,9 +499,7 @@
         if not last:
             near = operate_near(it + 1, image, leaf_len * (6 if it == 0 else 4) // 8)
             if ahead:
-                near_coef = coefs_of(f"near{it}", near)
-                if it == 0:
-                    prepare_mix()
+                near_coef = prepare_mix(near) if it == 0 else coefs_of(f"near{it}", near)
         else:
             for row in range(ITERS):
                 with phase(f"spread{row}"):
@@ -595,7 +597,7 @@
             pltpu.VMEM((128, leaf_len), bf16),
             pltpu.VMEM(u_factors.shape, f32),
             pltpu.VMEM(v_factors.shape, f32),
-            pltpu.VMEM((2 * padded, leaf_len), bf16),
+            pltpu.VMEM((2 * num_vectors + 2 * padded, leaf_len), bf16),
             pltpu.VMEM((2 * padded, leaf_len), bf16),
             pltpu.VMEM((leaf_len, 2 * padded), bf16),
             pltpu.VMEM((padded, 2 * padded), bf16),

time: 40.1 us -> 39.3 us (0.980)
  Pallas kernels: 37.1 us -> 36.2 us
    pallas_call x1, Pallas kernels: 37.1 us -> 36.2 us  [per_device(): pl.pallas_call(functools.partial(fused, size_gx, size_gy), out_shape=jax....]
where the time goes in v4:
time: 39.3 us; the launch traced here: 39.1 us
  Pallas kernels  36.2 us (92%)
  local copies, waits for them, and re-layouts  1.57 us (4%)
  between operations  1.31 us (3%)
    pallas_call x1, Pallas kernels, per_device(): pl.pallas_call(functools.partial(fused, size_gx, size_gy), out_shape=jax....  36.2 us
    unnamed x1, local copies, waits for them, and re-layouts  1.57 us

profile of v4, /device:TPU:0, one launch (start us, length us, event | category | flops | bytes accessed | tf_op | source)
XLA Modules:
  0.0 39.1 jit_solution(17717316660926997972)
XLA Ops:
  1.3 36.2 %gmres.1 = f32[16,2048]{1,0:T(8,128)} custom-call(f32[3,2048]{1,0:T(4,128)} %coords_hbm.1, f32[16,2048]{1,0:T(8,128)} %rhs_hbm.1, s32[1,2048]{1,0:T(1,128)} %order_hbm.1, s32[1]{0:T(128)S(6)} %copy.10.sizes_hbm, f32[3]{0:T(128)} %inv_hbm.1, f32[1]{0:T(128)S(6)} %copy.11.noise_hbm, f32[5,64,2048]{2,1,0:T(8,128)} %u_hbm.1, f32[5,64,2048]{2,1,0:T(8,128)} %v_hbm.1), custom_call_target="tpu_custom_call" | custom-call | tf_op jit(solution)/shard_map/gmres/pallas_call | solution.py:581
  37.5 1.6 %copy.12 = f32[16,2048]{1,0:T(8,128)} copy(f32[16,2048]{1,0:T(8,128)} %gmres.1) | data formatting | bytes 262144
